TPU v7x, 512 devices: a whole 4x8x8 slice. The times are simulated.
512 devices in a mesh: row: 16 (over x, z_hi, core), col: 32 (over z_lo, y).
Axes of the slice: x: 4, y: 8, z: 8 (z_hi: 2, z_lo: 4; z = z_hi * 4 + z_lo), core: 2. Of those that a mesh axis runs over, the one named last changes fastest.
Arguments:
- points: bfloat16 [12, 16, 512, 64], P(None, 'row', 'col'), may hold values from -7.5 to 7.5
- inverse_factor: bfloat16 [512, 512], replicated, as said below
- panel_index: int32 [1], replicated, may hold values from 15 to 95
- column_map: int32 [32], P('col'), may hold values from 0 to 31, each once
Outputs:
- panel: bfloat16 [6, 16, 512, 512], P(None, 'row', 'col')
- update: bfloat16 [6, 16, 512, 32, 512], P(None, 'row', None, 'col')
Inputs may be any that keep to these rules, and one draw needn't show every extreme that they name: `column_map`: a permutation of 0 .. 32 - 1. `inverse_factor`: zero above the diagonal.
All inputs are finite; a program needn't handle non-finite values.
Results may differ from a plain program's by a relative error of at most 0.0049.
Values may be sent and summed in bfloat16 or wider, within the bound.
A program may use at most 64 MiB of HBM per device.

v0:
```python
import jax
import jax.numpy as jnp
from jax import lax
from jax.sharding import PartitionSpec as P

RW = 6


JITTER = 1.0


def laid_out(pieces, dim):
    lengths = list(pieces.shape[1:])
    lengths[dim] *= pieces.shape[0]
    return jnp.moveaxis(pieces, 0, dim).reshape(lengths)


def from_everyone(x, axis):
    copies = jnp.broadcast_to(x, (lax.axis_size(axis), *x.shape))
    return lax.all_to_all(copies, axis, split_axis=0, concat_axis=0, tiled=True)


def gathered_copies(x, axis, dim):
    return laid_out(from_everyone(x, axis), dim)


def of_everyone(x, axis):
    return from_everyone(x, axis).astype(jnp.float32).sum(axis=0)


def kernel_tile(left_points, right_points):
    left_vals = left_points.astype(jnp.float32)
    right_vals = right_points.astype(jnp.float32)
    inner_products = lax.dot_general(
        left_points, right_points, (((1,), (1,)), ((), ())), preferred_element_type=jnp.float32
    )
    left_norms = jnp.sum(left_vals * left_vals, axis=1)
    right_norms = jnp.sum(right_vals * right_vals, axis=1)
    distance = left_norms[:, None] + right_norms[None, :] - 2.0 * inner_products
    return jnp.exp(-distance / (2.0 * left_points.shape[1]))


def panel_tile(row_points, panel_points, inverse_factor):
    rounded = kernel_tile(row_points, panel_points).astype(jnp.bfloat16)
    product = lax.dot_general(
        rounded, inverse_factor, (((1,), (1,)), ((), ())), preferred_element_type=jnp.float32
    )
    return product.astype(jnp.bfloat16)


def masked(values, keep):
    return jnp.where(keep, values.astype(jnp.float32), 0.0)


def shards(points, inverse_factor, panel_index, column_map):
    row_count = lax.axis_size("row")
    row_here = lax.axis_index("row")
    col_here = lax.axis_index("col")
    pivot_tile = panel_index[0]
    start_slot = (pivot_tile + row_count - row_here) // row_count
    local_points = lax.dynamic_slice_in_dim(points[:, 0], start_slot - 1, RW + 1, 0)
    blocks = gathered_copies(local_points, "col", 1)
    holds_panel = row_here == pivot_tile % row_count
    panel_points = (
        of_everyone(masked(blocks[0], holds_panel).astype(jnp.bfloat16), "row")
        .astype(jnp.float32)
        .astype(jnp.bfloat16)
    )
    window_points = blocks[1:]
    panel_full = jnp.stack(
        [
            panel_tile(window_points[window_slot], panel_points, inverse_factor)
            for window_slot in range(RW)
        ]
    )
    share_rows = local_points.shape[1]
    panel_part = lax.dynamic_slice_in_dim(panel_full, col_here * share_rows, share_rows, 1)
    column_tile = pivot_tile + 1 + column_map[0]
    holds_column = row_here == column_tile % row_count
    position = jnp.clip(column_tile // row_count - start_slot, 0, RW - 1)
    candidate_points = lax.dynamic_index_in_dim(window_points, position, 0, keepdims=False)
    column_points = (
        of_everyone(masked(candidate_points, holds_column).astype(jnp.bfloat16), "row")
        .astype(jnp.float32)
        .astype(jnp.bfloat16)
    )
    column_rows = panel_tile(column_points, panel_points, inverse_factor)
    identity = jnp.eye(inverse_factor.shape[0], dtype=jnp.float32)
    updates = []
    for window_slot in range(RW):
        tile_row = (start_slot + window_slot) * row_count + row_here
        update_tile = kernel_tile(window_points[window_slot], column_points)
        update_tile = update_tile + jnp.where(tile_row == column_tile, JITTER, 0.0) * identity
        update_tile = update_tile - lax.dot_general(
            panel_full[window_slot],
            column_rows,
            (((1,), (1,)), ((), ())),
            preferred_element_type=jnp.float32,
        )
        updates.append(update_tile.astype(jnp.bfloat16))
    update = jnp.stack(updates)[:, None, :, None, :]
    return (panel_part[:, None], update)


def solution(mesh):
    in_specs = (P(None, "row", "col", None), P(), P(), P("col"))
    out_specs = (P(None, "row", "col", None), P(None, "row", None, "col", None))
    return jax.shard_map(shards, mesh=mesh, in_specs=in_specs, out_specs=out_specs, check_vma=False)
```

profile of v0, /device:TPU:128, one launch (start us, length us, event | category | flops | bytes accessed | tf_op | source)
XLA Modules:
  0.0 134.5 jit_solution(6286223173983184873)
XLA Ops:
  0.6 0.0 copy-start
  1.4 0.8 dynamic-slice_bitcast_fusion.1
  2.1 0.1 broadcast_in_dim.17
  2.3 1.3 reshape.52
  3.6 11.4 %all-to-all-start = ((bf16[32,2,3584]{2,1,0:T(2,128)(2,1)}), bf16[32,2,3584]{2,1,0:T(2,128)(2,1)S(1)}, u32[]{:S(2)}, u32[]{:S(2)}) async-start(bf16[32,2,3584]{2,1,0:T(2,128)(2,1)} %reshape.52), calls=%async_computation | async-start | bytes 917504 | tf_op jit(solution)/shard_map/all_to_all | solution.py:20
  15.1 14.3 %all-to-all-done = bf16[32,2,3584]{2,1,0:T(2,128)(2,1)S(1)} async-done(((bf16[32,2,3584]{2,1,0:T(2,128)(2,1)}), bf16[32,2,3584]{2,1,0:T(2,128)(2,1)S(1)}, u32[]{:S(2)}, u32[]{:S(2)}) %all-to-all-start) | async-done | bytes 458784 | tf_op jit(solution)/shard_map/all_to_all | solution.py:20
  29.4 0.5 reshape.53
  30.0 1.1 multiply_reduce_fusion
  31.1 0.1 copy.12
  31.2 1.1 broadcast_in_dim.19
  32.2 10.2 %all-to-all-start.1 = ((bf16[16,512,64]{1,2,0:T(8,128)(2,1)}), bf16[16,512,64]{1,2,0:T(8,128)(2,1)S(1)}, u32[]{:S(2)}, u32[]{:S(2)}) async-start(bf16[16,512,64]{1,2,0:T(8,128)(2,1)} %broadcast_in_dim.19), calls=%async_computation.1 | async-start | bytes 2097152 | tf_op jit(solution)/shard_map/all_to_all | solution.py:20
  43.1 0.1 slice.62
  43.2 0.1 copy.13
  43.4 0.1 copy.14
  43.5 30.5 %all-to-all-done.1 = bf16[16,512,64]{1,2,0:T(8,128)(2,1)S(1)} async-done(((bf16[16,512,64]{1,2,0:T(8,128)(2,1)}), bf16[16,512,64]{1,2,0:T(8,128)(2,1)S(1)}, u32[]{:S(2)}, u32[]{:S(2)}) %all-to-all-start.1) | async-done | bytes 1048608 | tf_op jit(solution)/shard_map/all_to_all | solution.py:20
  74.0 1.1 broadcast_in_dim.22
  75.0 3.7 %all-to-all-start.2 = ((bf16[16,512,64]{1,2,0:T(8,128)(2,1)}), bf16[16,512,64]{1,2,0:T(8,128)(2,1)S(1)}, u32[]{:S(2)}, u32[]{:S(2)}) async-start(bf16[16,512,64]{1,2,0:T(8,128)(2,1)} %broadcast_in_dim.22), calls=%async_computation.2 | async-start | bytes 2097152 | tf_op jit(solution)/shard_map/all_to_all | solution.py:20
  78.7 1.4 %add.116 = f32[512]{0:T(512)} reshape(f32[32,16]{1,0:T(8,128)} %get-tuple-element.11) | data formatting | bytes 4096 | tf_op jit(solution)/shard_map/add | solution.py:39
  80.1 1.4 %add.234 = f32[512]{0:T(512)} reshape(f32[32,16]{1,0:T(8,128)} %get-tuple-element.12) | data formatting | bytes 4096 | tf_op jit(solution)/shard_map/add | solution.py:39
  81.5 1.4 %add.237 = f32[512]{0:T(512)} reshape(f32[32,16]{1,0:T(8,128)} %get-tuple-element.13) | data formatting | bytes 4096 | tf_op jit(solution)/shard_map/add | solution.py:39
  82.9 1.4 %add.240 = f32[512]{0:T(512)} reshape(f32[32,16]{1,0:T(8,128)} %get-tuple-element.14) | data formatting | bytes 4096 | tf_op jit(solution)/shard_map/add | solution.py:39
  84.3 1.4 %add.243 = f32[512]{0:T(512)} reshape(f32[32,16]{1,0:T(8,128)} %get-tuple-element.15) | data formatting | bytes 4096 | tf_op jit(solution)/shard_map/add | solution.py:39
  85.6 0.7 add.246
  86.3 0.9 fusion.133
  87.2 0.1 reduce_sum.99
  87.4 0.0 copy-start.10
  87.4 0.0 copy-start.25
  87.4 22.8 %all-to-all-done.2 = bf16[16,512,64]{1,2,0:T(8,128)(2,1)S(1)} async-done(((bf16[16,512,64]{1,2,0:T(8,128)(2,1)}), bf16[16,512,64]{1,2,0:T(8,128)(2,1)S(1)}, u32[]{:S(2)}, u32[]{:S(2)}) %all-to-all-start.2) | async-done | bytes 1048608 | tf_op jit(solution)/shard_map/all_to_all | solution.py:20
  110.3 0.1 reduce_sum.112
  110.5 0.7 convolution_convert_fusion
  111.2 1.6 %bitcast_dynamic-update-slice_fusion.5 = (bf16[6,512,512]{2,1,0:T(8,128)(2,1)}, bf16[512,512]{1,0:T(8,128)(2,1)}) fusion(bf16[512,512]{1,0:T(8,128)(2,1)S(1)} %copy-done, bf16[512,64]{1,0:T(8,128)(2,1)S(1)} %bitcast.122, bf16[512,64]{0,1:T(8,128)(2,1)S(1)} %reduce_sum.99, f32[512]{0:T(512)S(1)} %multiply_reduce_fusion.7, f32[512]{0:T(512)S(1)} %copy-done.29), kind=kOutput, calls=%fused_computation.122 | convolution fusion | flops 303824896 | bytes 1708032 | tf_op jit(solution)/shard_map/dot_general | solution.py:45
  112.8 0.0 copy-done.20
  112.8 0.4 fusion.30
  113.2 0.0 copy-start.11
  113.2 2.5 %bitcast_dynamic-update-slice_fusion.4 = (bf16[6,512,512]{2,1,0:T(8,128)(2,1)}, bf16[512,512]{1,0:T(8,128)(2,1)}) fusion(bf16[6,512,512]{2,1,0:T(8,128)(2,1)} %get-tuple-element.23, bf16[512,512]{1,0:T(8,128)(2,1)S(1)} %copy-done, bf16[512,64]{1,0:T(8,128)(2,1)S(1)} %bitcast.120, bf16[512,64]{0,1:T(8,128)(2,1)} %copy-done.10, f32[512]{0:T(512)S(1)} %copy-done.28, ...), kind=kOutput, calls=%fused_computation.121 | convolution fusion | flops 303824896 | bytes 1708032 | tf_op jit(solution)/shard_map/dot_general | solution.py:45
  115.7 0.4 fusion.37
  116.2 2.3 %bitcast_dynamic-update-slice_fusion.3 = (bf16[6,512,512]{2,1,0:T(8,128)(2,1)}, bf16[512,512]{1,0:T(8,128)(2,1)}) fusion(bf16[6,512,512]{2,1,0:T(8,128)(2,1)} %get-tuple-element.25, bf16[512,512]{1,0:T(8,128)(2,1)S(1)} %copy-done, bf16[512,64]{1,0:T(8,128)(2,1)S(1)} %bitcast.118, bf16[512,64]{0,1:T(8,128)(2,1)S(1)} %copy-done.11, f32[512]{0:T(512)S(1)} %copy-done.27, ...), kind=kOutput, calls=%fused_computation.120 | convolution fusion | flops 303824896 | bytes 1708032 | tf_op jit(solution)/shard_map/dot_general | solution.py:45
  118.5 1.4 %fusion.42 = f32[512,512]{1,0:T(8,128)} fusion(bf16[512,64]{1,0:T(8,128)(2,1)S(1)} %bitcast.119, bf16[512,64]{0,1:T(8,128)(2,1)S(1)} %copy-done.13, f32[]{:T(128)S(6)} %select_n.73, f32[512]{0:T(512)S(1)} %multiply_reduce_fusion.6, f32[512]{0:T(512)S(1)} %copy-done.27), kind=kOutput, calls=%fused_computation.61 | convolution fusion | flops 35651584 | bytes 1183748 | tf_op jit(solution)/shard_map/dot_general | solution.py:34
  119.8 0.0 copy-done.24
  119.8 0.0 copy-done.26
  119.8 1.6 %bitcast_dynamic-update-slice_fusion.2 = (bf16[6,512,512]{2,1,0:T(8,128)(2,1)}, bf16[512,512]{1,0:T(8,128)(2,1)}) fusion(bf16[6,512,512]{2,1,0:T(8,128)(2,1)} %get-tuple-element.27, bf16[512,512]{1,0:T(8,128)(2,1)S(1)} %copy-done, bf16[512,64]{1,0:T(8,128)(2,1)S(1)} %bitcast.116, bf16[512,64]{0,1:T(8,128)(2,1)S(1)} %copy-done.11, f32[512]{0:T(512)S(1)} %copy-done.24, ...), kind=kOutput, calls=%fused_computation.119 | convolution fusion | flops 303824896 | bytes 1708032 | tf_op jit(solution)/shard_map/dot_general | solution.py:45
  121.4 1.4 %fusion.47 = f32[512,512]{1,0:T(8,128)} fusion(bf16[512,64]{1,0:T(8,128)(2,1)S(1)} %bitcast.117, bf16[512,64]{0,1:T(8,128)(2,1)S(1)} %copy-done.13, f32[]{:T(128)S(6)} %select_n.74, f32[512]{0:T(512)S(1)} %multiply_reduce_fusion.6, f32[512]{0:T(512)S(1)} %copy-done.24), kind=kOutput, calls=%fused_computation.66 | convolution fusion | flops 35651584 | bytes 1183748 | tf_op jit(solution)/shard_map/dot_general | solution.py:34
  122.8 0.0 copy-done.15
  122.8 1.6 %bitcast_dynamic-update-slice_fusion.1 = (bf16[6,512,512]{2,1,0:T(8,128)(2,1)}, bf16[512,512]{1,0:T(8,128)(2,1)}) fusion(bf16[6,512,512]{2,1,0:T(8,128)(2,1)} %get-tuple-element.29, bf16[512,512]{1,0:T(8,128)(2,1)S(1)} %copy-done, bf16[512,64]{1,0:T(8,128)(2,1)S(1)} %bitcast.114, bf16[512,64]{0,1:T(8,128)(2,1)S(1)} %copy-done.11, f32[512]{0:T(512)S(1)} %copy-done.23, ...), kind=kOutput, calls=%fused_computation.118 | convolution fusion | flops 303824896 | bytes 1708032 | tf_op jit(solution)/shard_map/dot_general | solution.py:45
  124.4 1.3 fusion.52
  125.7 0.0 copy-done.22
  125.8 1.6 %bitcast_dynamic-update-slice_fusion = (bf16[6,512,512]{2,1,0:T(8,128)(2,1)}, bf16[512,512]{1,0:T(8,128)(2,1)}) fusion(bf16[6,512,512]{2,1,0:T(8,128)(2,1)} %get-tuple-element.31, bf16[512,512]{1,0:T(8,128)(2,1)S(1)} %copy-done, bf16[512,64]{1,0:T(8,128)(2,1)S(1)} %bitcast.112, bf16[512,64]{0,1:T(8,128)(2,1)S(1)} %copy-done.11, f32[512]{0:T(512)S(1)} %copy-done.22, ...), kind=kOutput, calls=%fused_computation.117 | convolution fusion | flops 303824896 | bytes 1708032 | tf_op jit(solution)/shard_map/dot_general | solution.py:45
  127.3 0.4 fusion.57
  127.7 1.7 %dynamic-slice_bitcast_fusion = bf16[6,1,16,512]{3,2,1,0:T(8,128)(2,1)} fusion(bf16[6,512,512]{2,1,0:T(8,128)(2,1)} %get-tuple-element.33, s32[]{:T(128)S(6)} %select_n.66), kind=kLoop, calls=%fused_computation.162 | loop fusion | bytes 196612 | tf_op jit(solution)/shard_map/broadcast_in_dim | solution.py:102
  129.4 0.5 fusion.82
  129.9 0.0 copy-start.2
  129.9 0.0 copy-start.7
  129.9 0.0 copy-done.5
  129.9 0.5 fusion.80
  130.4 0.5 fusion.78
  130.9 0.2 copy-done.2
  131.1 0.1 copy-done.7
  131.2 0.5 fusion.76
  131.7 0.0 copy-done.3
  131.7 0.1 copy-done.8
  131.9 0.5 fusion.74
  132.3 0.5 fusion.72
  132.8 0.0 copy-start.21
  132.8 1.7 %copy-done.21 = bf16[6,512,512]{2,1,0:T(8,128)(2,1)} copy-done((bf16[6,512,512]{2,1,0:T(8,128)(2,1)}, bf16[6,512,512]{2,1,0:T(8,128)(2,1)S(1)}, u32[]{:S(2)}) %copy-start.21) | copy-done | bytes 3145752
  (47 shorter events, 0.2 us)
Async XLA Ops:
  0.6 109.8 %copy-start = (bf16[512,512]{1,0:T(8,128)(2,1)S(1)}, bf16[512,512]{1,0:T(8,128)(2,1)}, u32[]{:S(2)}) copy-start(bf16[512,512]{1,0:T(8,128)(2,1)} %param.5) | copy-start | bytes 1572868
  3.6 25.8 %all-to-all-start = ((bf16[32,2,3584]{2,1,0:T(2,128)(2,1)}), bf16[32,2,3584]{2,1,0:T(2,128)(2,1)S(1)}, u32[]{:S(2)}, u32[]{:S(2)}) async-start(bf16[32,2,3584]{2,1,0:T(2,128)(2,1)} %reshape.52), calls=%async_computation | async-start | bytes 917504 | tf_op jit(solution)/shard_map/all_to_all | solution.py:20
  32.2 41.7 %all-to-all-start.1 = ((bf16[16,512,64]{1,2,0:T(8,128)(2,1)}), bf16[16,512,64]{1,2,0:T(8,128)(2,1)S(1)}, u32[]{:S(2)}, u32[]{:S(2)}) async-start(bf16[16,512,64]{1,2,0:T(8,128)(2,1)} %broadcast_in_dim.19), calls=%async_computation.1 | async-start | bytes 2097152 | tf_op jit(solution)/shard_map/all_to_all | solution.py:20
  75.0 35.2 %all-to-all-start.2 = ((bf16[16,512,64]{1,2,0:T(8,128)(2,1)}), bf16[16,512,64]{1,2,0:T(8,128)(2,1)S(1)}, u32[]{:S(2)}, u32[]{:S(2)}) async-start(bf16[16,512,64]{1,2,0:T(8,128)(2,1)} %broadcast_in_dim.22), calls=%async_computation.2 | async-start | bytes 2097152 | tf_op jit(solution)/shard_map/all_to_all | solution.py:20
  86.3 24.9 %copy-start.29 = (f32[512]{0:T(512)S(1)}, f32[512]{0:T(512)}, u32[]{:S(2)}) copy-start(f32[512]{0:T(512)} %add.116) | copy-start | bytes 6148
  87.2 24.0 %copy-start.19 = (bf16[1,32,16,64]{3,2,0,1:T(8,128)(2,1)S(1)}, bf16[1,32,16,64]{3,2,0,1:T(8,128)(2,1)}, u32[]{:S(2)}) copy-start(bf16[1,32,16,64]{3,2,0,1:T(8,128)(2,1)} %get-tuple-element.21) | copy-start | bytes 196612
  87.4 23.8 %copy-start.10 = (bf16[512,64]{0,1:T(8,128)(2,1)}, bf16[512,64]{0,1:T(8,128)(2,1)S(1)}, u32[]{:S(2)}) copy-start(bf16[512,64]{0,1:T(8,128)(2,1)S(1)} %reduce_sum.99) | copy-start | bytes 196612
  87.4 25.8 %copy-start.25 = (f32[512]{0:T(512)}, f32[512]{0:T(512)S(1)}, u32[]{:S(2)}) copy-start(f32[512]{0:T(512)S(1)} %multiply_reduce_fusion.7) | copy-start | bytes 6148
  110.4 2.4 %copy-start.12 = (bf16[512,64]{0,1:T(8,128)(2,1)}, bf16[512,64]{0,1:T(8,128)(2,1)S(1)}, u32[]{:S(2)}) copy-start(bf16[512,64]{0,1:T(8,128)(2,1)S(1)} %reduce_sum.112) | copy-start | bytes 196612
  110.5 2.3 %copy-start.20 = (bf16[1,32,16,64]{3,2,0,1:T(8,128)(2,1)S(1)}, bf16[1,32,16,64]{3,2,0,1:T(8,128)(2,1)}, u32[]{:S(2)}) copy-start(bf16[1,32,16,64]{3,2,0,1:T(8,128)(2,1)} %get-tuple-element.21) | copy-start | bytes 196612
  110.5 2.3 %copy-start.30 = (f32[512]{0:T(512)S(1)}, f32[512]{0:T(512)}, u32[]{:S(2)}) copy-start(f32[512]{0:T(512)} %add.116) | copy-start | bytes 6148
  111.1 2.1 %copy-start.18 = (bf16[1,32,16,64]{3,2,0,1:T(8,128)(2,1)S(1)}, bf16[1,32,16,64]{3,2,0,1:T(8,128)(2,1)}, u32[]{:S(2)}) copy-start(bf16[1,32,16,64]{3,2,0,1:T(8,128)(2,1)} %get-tuple-element.20) | copy-start | bytes 196612
  111.2 2.1 %copy-start.28 = (f32[512]{0:T(512)S(1)}, f32[512]{0:T(512)}, u32[]{:S(2)}) copy-start(f32[512]{0:T(512)} %add.234) | copy-start | bytes 6148
  113.2 2.6 %copy-start.13 = (bf16[512,64]{0,1:T(8,128)(2,1)S(1)}, bf16[512,64]{0,1:T(8,128)(2,1)}, u32[]{:S(2)}) copy-start(bf16[512,64]{0,1:T(8,128)(2,1)} %copy-done.12) | copy-start | bytes 196612
  113.2 3.0 %copy-start.11 = (bf16[512,64]{0,1:T(8,128)(2,1)S(1)}, bf16[512,64]{0,1:T(8,128)(2,1)}, u32[]{:S(2)}) copy-start(bf16[512,64]{0,1:T(8,128)(2,1)} %copy-done.10) | copy-start | bytes 196612
  113.2 3.0 %copy-start.17 = (bf16[1,32,16,64]{3,2,0,1:T(8,128)(2,1)S(1)}, bf16[1,32,16,64]{3,2,0,1:T(8,128)(2,1)}, u32[]{:S(2)}) copy-start(bf16[1,32,16,64]{3,2,0,1:T(8,128)(2,1)} %get-tuple-element.19) | copy-start | bytes 196612
  113.2 3.0 %copy-start.27 = (f32[512]{0:T(512)S(1)}, f32[512]{0:T(512)}, u32[]{:S(2)}) copy-start(f32[512]{0:T(512)} %add.237) | copy-start | bytes 6148
  116.1 3.7 %copy-start.16 = (bf16[1,32,16,64]{3,2,0,1:T(8,128)(2,1)S(1)}, bf16[1,32,16,64]{3,2,0,1:T(8,128)(2,1)}, u32[]{:S(2)}) copy-start(bf16[1,32,16,64]{3,2,0,1:T(8,128)(2,1)} %get-tuple-element.18) | copy-start | bytes 196612
  116.1 3.7 %copy-start.24 = (f32[512]{0:T(512)S(1)}, f32[512]{0:T(512)}, u32[]{:S(2)}) copy-start(f32[512]{0:T(512)} %add.240) | copy-start | bytes 6148
  116.1 3.7 %copy-start.26 = (f32[512]{0:T(512)S(1)}, f32[512]{0:T(512)}, u32[]{:S(2)}) copy-start(f32[512]{0:T(512)} %copy-done.25) | copy-start | bytes 6148
  119.8 3.0 %copy-start.15 = (bf16[1,32,16,64]{3,2,0,1:T(8,128)(2,1)S(1)}, bf16[1,32,16,64]{3,2,0,1:T(8,128)(2,1)}, u32[]{:S(2)}) copy-start(bf16[1,32,16,64]{3,2,0,1:T(8,128)(2,1)} %get-tuple-element.17) | copy-start | bytes 196612
  119.8 3.0 %copy-start.23 = (f32[512]{0:T(512)S(1)}, f32[512]{0:T(512)}, u32[]{:S(2)}) copy-start(f32[512]{0:T(512)} %add.243) | copy-start | bytes 6148
  122.8 3.0 %copy-start.14 = (bf16[1,32,16,64]{3,2,0,1:T(8,128)(2,1)S(1)}, bf16[1,32,16,64]{3,2,0,1:T(8,128)(2,1)}, u32[]{:S(2)}) copy-start(bf16[1,32,16,64]{3,2,0,1:T(8,128)(2,1)} %get-tuple-element.16) | copy-start | bytes 196612
  122.8 3.0 %copy-start.22 = (f32[512]{0:T(512)S(1)}, f32[512]{0:T(512)}, u32[]{:S(2)}) copy-start(f32[512]{0:T(512)} %add.246) | copy-start | bytes 6148
  127.3 2.1 %copy-start.4 = (bf16[512,512]{1,0:T(8,128)(2,1)S(1)}, bf16[512,512]{1,0:T(8,128)(2,1)}, u32[]{:S(2)}) copy-start(bf16[512,512]{1,0:T(8,128)(2,1)} %get-tuple-element.24) | copy-start | bytes 1572868
  127.3 2.6 %copy-start.5 = (bf16[512,512]{1,0:T(8,128)(2,1)S(1)}, bf16[512,512]{1,0:T(8,128)(2,1)}, u32[]{:S(2)}) copy-start(bf16[512,512]{1,0:T(8,128)(2,1)} %get-tuple-element.26) | copy-start | bytes 1572868
  127.7 2.7 %copy-start.1 = (f32[512,512]{1,0:T(8,128)S(1)}, f32[512,512]{1,0:T(8,128)}, u32[]{:S(2)}) copy-start(f32[512,512]{1,0:T(8,128)} %fusion.42) | copy-start | bytes 3145732
  127.7 2.7 %copy-start.6 = (bf16[512,512]{1,0:T(8,128)(2,1)S(1)}, bf16[512,512]{1,0:T(8,128)(2,1)}, u32[]{:S(2)}) copy-start(bf16[512,512]{1,0:T(8,128)(2,1)} %get-tuple-element.28) | copy-start | bytes 1572868
  129.9 1.2 copy-start.2
  129.9 1.3 %copy-start.7 = (bf16[512,512]{1,0:T(8,128)(2,1)S(1)}, bf16[512,512]{1,0:T(8,128)(2,1)}, u32[]{:S(2)}) copy-start(bf16[512,512]{1,0:T(8,128)(2,1)} %get-tuple-element.30) | copy-start | bytes 1572868
  130.4 1.3 copy-start.3
  130.4 1.5 %copy-start.8 = (bf16[512,512]{1,0:T(8,128)(2,1)S(1)}, bf16[512,512]{1,0:T(8,128)(2,1)}, u32[]{:S(2)}) copy-start(bf16[512,512]{1,0:T(8,128)(2,1)} %get-tuple-element.32) | copy-start | bytes 1572868
  130.9 1.4 %copy-start.9 = (bf16[512,512]{1,0:T(8,128)(2,1)S(1)}, bf16[512,512]{1,0:T(8,128)(2,1)}, u32[]{:S(2)}) copy-start(bf16[512,512]{1,0:T(8,128)(2,1)} %get-tuple-element.34) | copy-start | bytes 1572868
  132.8 1.7 %copy-start.21 = (bf16[6,512,512]{2,1,0:T(8,128)(2,1)}, bf16[6,512,512]{2,1,0:T(8,128)(2,1)S(1)}, u32[]{:S(2)}) copy-start(bf16[6,512,512]{2,1,0:T(8,128)(2,1)S(1)} %fusion.72) | copy-start | bytes 9437188
where the time goes:
time: 135 us; the launch traced here: 134 us
  waiting for transfers between devices  67.6 us (50%)
  starting transfers between devices  25.2 us (19%)
  matrix products  19.8 us (15%)
  local copies, waits for them, and re-layouts  17.8 us (13%)
  between operations  2.62 us (2%)
  other arithmetic  1.48 us (1%)
    all_to_all x3, waiting for transfers between devices, from_everyone(): return lax.all_to_all(copies, axis, split_axis=0, concat_axis=0, tiled=True)  67.6 us
    all_to_all x3, starting transfers between devices, from_everyone(): return lax.all_to_all(copies, axis, split_axis=0, concat_axis=0, tiled=True)  25.2 us
    dot_general x7, matrix products, panel_tile(): lax.dot_general(rounded, inverse_factor, (((1,), (1,)), ((), ())), prefer...  11.8 us
    add x6, local copies, waits for them, and re-layouts, kernel_tile(): distance = left_norms[:, None] + right_norms[None, :] - 2.0 * inner_products  7.56 us
    dot_general x6, matrix products, kernel_tile(): lax.dot_general(left_points, right_points, (((1,), (1,)), ((), ())), pref...  5.18 us
    unnamed x64, local copies, waits for them, and re-layouts  4.14 us
    dot_general x6, matrix products, shards(): lax.dot_general(panel_full[window_slot], column_rows, (((1,), (1,)), ((),...  2.81 us
  transfers between devices with their start and end apart: 3, of which 3 were waited for; matrix products, arithmetic and copies ran while one was open for 7% of the time, Pallas kernels for 0%

commit v1 on v0

v1 whole, which is shorter than its diff:
```python
import math

import jax
import jax.numpy as jnp
from jax import lax
from jax.experimental import pallas as pl
from jax.experimental.pallas import tpu as pltpu
from jax.sharding import PartitionSpec as P

RW = 6
JITTER = 1.0
NB = 512
DIM = 64
N_ROW = 16
NX, NZH, NCORE, NZL, NY = 4, 2, 2, 4, 8
NZ = NZH * NZL
NP = NX * NCORE
SCALE = math.log2(math.e) / DIM
MESH = pl.DeviceIdType.MESH
BF = jnp.bfloat16
F32 = jnp.float32


def first_slot(p, r):
    return (p + N_ROW - r) // N_ROW


def gather_kernel(
    p_ref, cm_ref, pts_ref, wb, zb,
    xe, xb, ps, yc, yp, cms, zs,
    x_s, x_r, c_s, c_r, wy_s, wy_r, wz_s, wz_r, w2y_s, w2y_r, w2z_s, w2z_r,
    yc_s, yc_r, yp_s, yp_r, z_s, z_r, sw_s, sw_r,
):
    row, col = lax.axis_index("row"), lax.axis_index("col")
    x, zh, core = row // 4, (row // 2) % 2, row % 2
    zl, y = col // NY, col % NY
    z = zh * NZL + zl
    q = x * 2 + core
    p = p_ref[0]

    def dev(x_=x, zh_=zh, core_=core, zl_=zl, y_=y):
        return ((x_ * 2 + zh_) * 2 + core_, zl_ * NY + y_)

    def q_dev(q_):
        return dev(x_=q_ // 2, core_=q_ % 2)

    def z_dev(z_):
        return dev(zh_=z_ // NZL, zl_=z_ % NZL)

    q_peers = [(q + d) % NP for d in range(1, NP)]
    y_peers = [(y + d) % NY for d in range(1, NY)]
    z_peers = [(z + d) % NZ for d in range(1, NZ)]
    l_peers = [(zl + d) % NZL for d in range(1, NZL)]

    barrier = pltpu.get_barrier_semaphore()
    for q_ in q_peers:
        pl.semaphore_signal(barrier, 1, device_id=q_dev(q_), device_id_type=MESH)
    for y_ in y_peers:
        pl.semaphore_signal(barrier, 1, device_id=dev(y_=y_), device_id_type=MESH)
    for z_ in z_peers:
        pl.semaphore_signal(barrier, 1, device_id=z_dev(z_), device_id_type=MESH)

    base = jnp.clip(first_slot(p, row) - 1, 0, pts_ref.shape[0] - RW - 1)
    for t in range(3):
        wb[t, zl, y] = jnp.concatenate([pts_ref[base + 1 + t, 0], pts_ref[base + 4 + t, 0]], axis=1)
    first = pts_ref[base + 1, 0].astype(F32)
    second = pts_ref[base + 2, 0].astype(F32)
    pivot = pts_ref[base, 0].astype(F32)
    cand = jnp.concatenate([first, second], axis=1)
    piv = jnp.concatenate([jnp.zeros_like(pivot), pivot], axis=1)
    for h in range(2):
        rows = slice(8 * h, 8 * h + 8)
        xe[h, 0] = cand[rows].astype(BF)
        xe[h, 1] = piv[rows].astype(BF)
    xb[q] = xe[core]
    cms[zl] = jnp.full((8, 128), cm_ref[0], jnp.int32).astype(F32)
    pl.semaphore_wait(barrier, len(q_peers) + len(y_peers) + len(z_peers))

    sends = []

    def send(src, dst, ssem, rsem, to):
        copy = pltpu.make_async_remote_copy(
            src_ref=src, dst_ref=dst, send_sem=ssem, recv_sem=rsem, device_id=to, device_id_type=MESH
        )
        copy.start()
        sends.append(copy)

    def arrived(dst, rsem):
        pltpu.make_async_remote_copy(
            src_ref=dst, dst_ref=dst, send_sem=rsem, recv_sem=rsem, device_id=dev(), device_id_type=MESH
        ).wait_recv()

    for q_ in q_peers:
        send(xe.at[q_ % 2], xb.at[q], x_s.at[q_], x_r.at[q], q_dev(q_))
    for l_ in l_peers:
        send(cms.at[zl], cms.at[zl], c_s.at[l_], c_r.at[zl], dev(zl_=l_))
    for y_ in y_peers:
        send(wb.at[pl.ds(0, 2), zl, y], wb.at[pl.ds(0, 2), zl, y], wy_s.at[y_], wy_r.at[y], dev(y_=y_))
    for l_ in l_peers:
        send(wb.at[2, zl, y], wb.at[2, zl, y], wz_s.at[l_], wz_r.at[zl], dev(zl_=l_))

    for q_ in q_peers:
        arrived(xb.at[q_], x_r.at[q_])
    mine = jnp.zeros((8, 128), F32)
    for k in range(NP):
        r = ((k // 2) * 2 + zh) * 2 + k % 2
        mine += jnp.where(r == p % N_ROW, xb[k, 1].astype(F32), 0.0)
    ps[...] = mine.astype(BF)
    for y_ in y_peers:
        send(xb.at[:, 0], yc.at[y], yc_s.at[y_], yc_r.at[y], dev(y_=y_))
    yp[y] = mine.astype(BF)
    yc[y] = xb[:, 0]
    for y_ in y_peers:
        send(ps, yp.at[y], yp_s.at[y_], yp_r.at[y], dev(y_=y_))

    for l_ in l_peers:
        arrived(wb.at[2, l_, y], wz_r.at[l_])
    for y_ in y_peers:
        send(wb.at[2, :, y], wb.at[2, :, y], w2y_s.at[y_], w2y_r.at[y], dev(y_=y_))
    for y_ in y_peers:
        arrived(wb.at[pl.ds(0, 2), zl, y_], wy_r.at[y_])
    for l_ in l_peers:
        send(wb.at[pl.ds(0, 2), zl], wb.at[pl.ds(0, 2), zl], w2z_s.at[l_], w2z_r.at[zl], dev(zl_=l_))

    for l_ in l_peers:
        arrived(cms.at[l_], c_r.at[l_])
    for y_ in y_peers:
        arrived(yc.at[y_], yc_r.at[y_])
        arrived(yp.at[y_], yp_r.at[y_])
    lower = lax.broadcasted_iota(jnp.int32, (8, 128), 1) < DIM
    wanted = [cms[l_] for l_ in range(NZL)]
    ranks = []
    for k in range(NP):
        r = ((k // 2) * 2 + zh) * 2 + k % 2
        own = first_slot(p, r) * N_ROW + r - p - 1
        both = jnp.where(lower, own, own + N_ROW).astype(F32)
        ranks.append(both)
    for y_ in range(NY):
        tiles = [yc[y_, k].astype(F32) for k in range(NP)]
        pivot_tile = yp[y_].astype(F32)
        for l_ in range(NZL):
            total = jnp.zeros((8, 128), F32)
            for k in range(NP):
                total = jnp.where(wanted[l_] == ranks[k], tiles[k], total)
            folded = total + pltpu.roll(total, DIM, 1)
            zs[l_, y_] = jnp.where(lower, folded, pivot_tile).astype(BF)
    for z_ in z_peers:
        send(zs.at[z_ % NZL], zb.at[core, z], z_s.at[z_], z_r.at[z], z_dev(z_))
    zb[core, z] = zs[zl]
    other = 1 - core
    for z_ in z_peers:
        arrived(zb.at[core, z_], z_r.at[z_])
        send(zb.at[core, z_], zb.at[core, z_], sw_s.at[z_], sw_r.at[z_], dev(core_=other))
    send(zb.at[core, z], zb.at[core, z], sw_s.at[z], sw_r.at[z], dev(core_=other))

    for l_ in l_peers:
        arrived(wb.at[pl.ds(0, 2), l_], w2z_r.at[l_])
    for y_ in y_peers:
        arrived(wb.at[2, :, y_], w2y_r.at[y_])
    for z_ in range(NZ):
        arrived(zb.at[other, z_], sw_r.at[z_])
    for copy in sends:
        copy.wait_send()


def gathered(panel_index, column_map, points):
    vmem = pl.BlockSpec(memory_space=pltpu.VMEM)
    smem = pl.BlockSpec(memory_space=pltpu.SMEM)
    dma = pltpu.SemaphoreType.DMA
    counts = [NP, NP, NZL, NZL, NY, NY, NZL, NZL, NY, NY, NZL, NZL, NY, NY, NY, NY, NZ, NZ, NZ, NZ]
    return pl.pallas_call(
        gather_kernel,
        out_shape=[
            jax.ShapeDtypeStruct((3, NZL, NY, 16, 128), BF),
            jax.ShapeDtypeStruct((2, NZ, NY, 8, 128), BF),
        ],
        in_specs=[smem, smem, vmem],
        out_specs=[vmem, vmem],
        scratch_shapes=[
            pltpu.VMEM((2, 2, 8, 128), BF),
            pltpu.VMEM((NP, 2, 8, 128), BF),
            pltpu.VMEM((8, 128), BF),
            pltpu.VMEM((NY, NP, 8, 128), BF),
            pltpu.VMEM((NY, 8, 128), BF),
            pltpu.VMEM((NZL, 8, 128), F32),
            pltpu.VMEM((NZL, NY, 8, 128), BF),
        ]
        + [dma((n,)) for n in counts],
        compiler_params=pltpu.CompilerParams(collective_id=0, has_side_effects=True),
        name="gather_points",
    )(panel_index, column_map, points)


def dot(a, b):
    return lax.dot_general(a, b, (((1,), (0,)), ((), ())), preferred_element_type=F32)


def dot_t(a, b):
    return lax.dot_general(a, b, (((1,), (1,)), ((), ())), preferred_element_type=F32)


def tiles_kernel(p_ref, cm_ref, wb, zb, inv, panel_out, update_out, rhs, bias, lcol, panel):
    slot = pl.program_id(0)
    row, col = lax.axis_index("row"), lax.axis_index("col")
    p = p_ref[0]
    half_rows = NB // 2

    @pl.when(slot == 0)
    def _():
        parts = []
        for h in range(2):
            parts.append(zb[h, 0:NZL].astype(F32) + zb[h, NZL:NZ].astype(F32))
        both = jnp.stack(parts, axis=2).reshape(NB, 128)
        flipped = both.T
        squares = flipped * flipped
        for k in range(2):
            one = flipped[k * DIM : (k + 1) * DIM].astype(BF)
            none = jnp.zeros_like(one)
            rhs[0, k] = jnp.concatenate([one, none], axis=0)
            rhs[1, k] = jnp.concatenate([none, one], axis=0)
            bias[k] = jnp.broadcast_to(
                jnp.sum(squares[k * DIM : (k + 1) * DIM], axis=0, keepdims=True) * (0.5 * SCALE), (8, NB)
            )
        lanes = lax.broadcasted_iota(jnp.int32, (NB, 128), 1)
        pivots = both.astype(BF)
        norm = jnp.sum(jnp.where(lanes >= DIM, both * both, 0.0), axis=1, keepdims=True) * (0.5 * SCALE)
        cross = jnp.exp2(SCALE * dot(pivots, rhs[1, 0]) - norm - bias[0, 0:1])
        cross = cross.astype(BF)
        lcol[0:half_rows] = dot(inv[0:half_rows, 0:half_rows], cross[0:half_rows]).astype(BF)
        lcol[half_rows:NB] = dot(inv[half_rows:NB], cross).astype(BF)

    which, half = slot % 3, slot // 3
    tile_row = (first_slot(p, row) + slot) * N_ROW + row
    jitter = jnp.where(tile_row == p + 1 + cm_ref[0], JITTER, 0.0)
    eye = lax.broadcasted_iota(jnp.int32, (128, 128), 0) == lax.broadcasted_iota(jnp.int32, (128, 128), 1)
    diagonal = jnp.where(eye, jitter, 0.0)
    low_lane = half * DIM
    for m in range(2):
        rows = slice(m * half_rows, (m + 1) * half_rows)
        here = wb[which, rows]
        vals = here.astype(F32)
        lanes = lax.broadcasted_iota(jnp.int32, (half_rows, 128), 1)
        inside = (lanes >= low_lane) & (lanes < low_lane + DIM)
        norm = jnp.sum(jnp.where(inside, vals * vals, 0.0), axis=1, keepdims=True) * (0.5 * SCALE)
        kpanel = jnp.exp2(SCALE * dot(here, rhs[half, 1]) - norm - bias[1, 0:1]).astype(BF)
        panel[rows, 0:half_rows] = dot_t(kpanel[:, 0:half_rows], inv[0:half_rows, 0:half_rows]).astype(BF)
        panel[rows, half_rows:NB] = dot_t(kpanel, inv[half_rows:NB]).astype(BF)
        tile = jnp.exp2(SCALE * dot(here, rhs[half, 0]) - norm - bias[0, 0:1])
        product = dot(panel[rows], lcol[...])
        for i in range(2):
            sub = slice(i * 128, (i + 1) * 128)
            out_rows = slice(m * half_rows + i * 128, m * half_rows + (i + 1) * 128)
            for j in range(4):
                cols = slice(j * 128, (j + 1) * 128)
                value = tile[sub, cols]
                if j == 2 * m + i:
                    value = value + diagonal
                update_out[0, out_rows, cols] = (value - product[sub, cols]).astype(BF)
    start = pl.multiple_of(col * 16, 16)
    panel_out[slot] = panel[pl.ds(start, 16)]


def tiles(panel_index, column_map, wb, zb, inverse_factor):
    smem = pl.BlockSpec(memory_space=pltpu.SMEM)

    def whole(shape):
        return pl.BlockSpec(shape, lambda i: (0,) * len(shape))

    flops = 2 * NB * NB * (RW * (2 * 128 + 2 * NB) + 2 * NB)
    return pl.pallas_call(
        tiles_kernel,
        grid=(RW,),
        out_shape=[
            jax.ShapeDtypeStruct((RW, 16, NB), BF),
            jax.ShapeDtypeStruct((RW, NB, NB), BF),
        ],
        in_specs=[smem, smem, whole((3, NB, 128)), whole((2, NZ, NY, 8, 128)), whole((NB, NB))],
        out_specs=[whole((RW, 16, NB)), pl.BlockSpec((1, NB, NB), lambda i: (i, 0, 0))],
        scratch_shapes=[
            pltpu.VMEM((2, 2, 128, NB), BF),
            pltpu.VMEM((2, 8, NB), F32),
            pltpu.VMEM((NB, NB), BF),
            pltpu.VMEM((NB, NB), BF),
        ],
        cost_estimate=pl.CostEstimate(flops=flops, bytes_accessed=5 << 20, transcendentals=13 * NB * NB),
        name="window_tiles",
    )(panel_index, column_map, wb, zb, inverse_factor)


def shards(points, inverse_factor, panel_index, column_map):
    wb, zb = gathered(panel_index, column_map, points)
    panel_part, update = tiles(panel_index, column_map, wb.reshape(3, NB, 128), zb, inverse_factor)
    return panel_part[:, None], update[:, None, :, None, :]


def solution(mesh):
    in_specs = (P(None, "row", "col", None), P(), P(), P("col"))
    out_specs = (P(None, "row", "col", None), P(None, "row", None, "col", None))
    return jax.shard_map(shards, mesh=mesh, in_specs=in_specs, out_specs=out_specs, check_vma=False)
```

time: 135 us -> 47.9 us (0.35)
  the two profiles are of different devices: /device:TPU:128 before, /device:TPU:1 now
where the time goes in v1:
time: 47.9 us; the launch traced here: 47.7 us
  Pallas kernels  45.7 us (95%)
  between operations  1.93 us (4%)
    pallas_call x1, Pallas kernels, gathered(): pl.pallas_call(gather_kernel, out_shape=[jax.ShapeDtypeStruct((3, NZL, NY...  36.3 us
    pallas_call x1, Pallas kernels, tiles(): pl.pallas_call(tiles_kernel, grid=(RW,), out_shape=[jax.ShapeDtypeStruct(...  9.45 us

profile of v1, /device:TPU:1, one launch (start us, length us, event | category | flops | bytes accessed | tf_op | source)
XLA Modules:
  0.0 47.7 jit_solution(16890789113629449214)
XLA Ops:
  1.9 36.3 %gather_points.1 = (bf16[3,4,8,16,128]{4,3,2,1,0:T(8,128)(2,1)}, bf16[2,8,8,8,128]{4,3,2,1,0:T(8,128)(2,1)}) custom-call(s32[1]{0:T(128)S(6)} %copy.8.p_ref, s32[1]{0:T(128)S(6)} %copy.9.cm_ref, bf16[12,1,16,64]{3,2,1,0:T(8,128)(2,1)} %pts_ref.1), custom_call_target="tpu_custom_call" | custom-call | tf_op jit(solution)/shard_map/gather_points/pallas_call | solution.py:171
  38.2 9.4 %window_tiles.1 = (bf16[6,16,512]{2,1,0:T(8,128)(2,1)}, bf16[6,512,512]{2,1,0:T(8,128)(2,1)}) custom-call(s32[1]{0:T(128)S(6)} %copy.8.p_ref, s32[1]{0:T(128)S(6)} %copy.9.cm_ref, bf16[3,512,128]{2,1,0:T(8,128)(2,1)} %bitcast.7, bf16[2,8,8,8,128]{4,3,2,1,0:T(8,128)(2,1)} %get-tuple-element.7.zb, bf16[512,512]{1,0:T(8,128)(2,1)} %inv.1), custom_call_target="tpu_custom_call" | custom-call | flops 4563402752 | bytes 5242880 | tf_op jit(solution)/shard_map/window_tiles/pallas_call | solution.py:270

commit v2 on v1

v2 whole, which is shorter than its diff:
```python
import math

import jax
import jax.numpy as jnp
from jax import lax
from jax.experimental import pallas as pl
from jax.experimental.pallas import tpu as pltpu
from jax.sharding import PartitionSpec as P

RW = 6
JITTER = 1.0
NB = 512
DIM = 64
N_ROW = 16
NX, NZH, NCORE, NZL, NY = 4, 2, 2, 4, 8
NZ = NZH * NZL
NP = NX * NCORE
SCALE = math.log2(math.e) / DIM
MESH = pl.DeviceIdType.MESH
BF = jnp.bfloat16
F32 = jnp.float32


def first_slot(p, r):
    return (p + N_ROW - r) // N_ROW


def assembled(buf):
    low = lax.broadcasted_iota(jnp.int32, (8, 128), 1) < DIM
    parts = []
    for h in range(2):
        packed = buf[h, 0:NZL].astype(F32) + buf[h, NZL:NZ].astype(F32)
        turned = pltpu.roll(packed.reshape(NZL * 4 * 8, 128), DIM, 1).reshape(packed.shape)
        parts.append(jnp.where(low, jnp.concatenate([packed, turned], axis=1), 0.0))
    return jnp.stack(parts, axis=2).reshape(NB, 128)


def packed_pair(a, b, low):
    return jnp.where(low, a, pltpu.roll(b, DIM, 1))


def fill_rhs(block, rhs, bias):
    turned = block.T[0:DIM]
    one = turned.astype(BF)
    none = jnp.zeros_like(one)
    rhs[0] = jnp.concatenate([one, none], axis=0)
    rhs[1] = jnp.concatenate([none, one], axis=0)
    norm = jnp.sum(turned * turned, axis=0, keepdims=True) * (0.5 * SCALE)
    bias[...] = jnp.broadcast_to(norm, (8, NB))


def row_norm(vals, low_lane):
    lanes = lax.broadcasted_iota(jnp.int32, vals.shape, 1)
    inside = (lanes >= low_lane) & (lanes < low_lane + DIM)
    return jnp.sum(jnp.where(inside, vals * vals, 0.0), axis=1, keepdims=True) * (0.5 * SCALE)


def dot(a, b):
    return lax.dot_general(a, b, (((1,), (0,)), ((), ())), preferred_element_type=F32)


def dot_t(a, b):
    return lax.dot_general(a, b, (((1,), (1,)), ((), ())), preferred_element_type=F32)


def gather_kernel(
    p_hbm, cm_hbm, pts_hbm, inv_hbm, wb, zc, xp, panel, inv,
    p_ref, cm_ref, pts_ref, xe, xb, ps, yc, yp, cms, zs, zq, zp, rhs, bias,
    x_s, x_r, c_s, c_r, wy_s, wy_r, wz_s, wz_r, w2y_s, w2y_r, w2z_s, w2z_r,
    yc_s, yc_r, yp_s, yp_r, zp_s, zp_r, zc_s, zc_r, in_s,
):
    row, col = lax.axis_index("row"), lax.axis_index("col")
    x, zh, core = row // 4, (row // 2) % 2, row % 2
    zl, y = col // NY, col % NY
    z = zh * NZL + zl
    q = x * 2 + core

    def dev(x_=x, zh_=zh, core_=core, zl_=zl, y_=y):
        return ((x_ * 2 + zh_) * 2 + core_, zl_ * NY + y_)

    def q_dev(q_):
        return dev(x_=q_ // 2, core_=q_ % 2)

    def z_dev(z_, core_):
        return dev(zh_=z_ // NZL, zl_=z_ % NZL, core_=core_)

    q_peers = [(q + d) % NP for d in range(1, NP)]
    y_peers = [(y + d) % NY for d in range(1, NY)]
    z_peers = [(z + d) % NZ for d in range(1, NZ)]
    l_peers = [(zl + d) % NZL for d in range(1, NZL)]
    line = [(z_, (core + k) % 2) for z_ in z_peers for k in range(2)] + [(z, 1 - core)]

    barrier = pltpu.get_barrier_semaphore()
    for q_ in q_peers:
        pl.semaphore_signal(barrier, 1, device_id=q_dev(q_), device_id_type=MESH)
    for y_ in y_peers:
        pl.semaphore_signal(barrier, 1, device_id=dev(y_=y_), device_id_type=MESH)
    for z_, k_ in line[:-1]:
        pl.semaphore_signal(barrier, 1, device_id=z_dev(z_, k_), device_id_type=MESH)

    loads = [
        pltpu.make_async_copy(src, dst, in_s.at[i])
        for i, (src, dst) in enumerate(
            [(p_hbm, p_ref), (cm_hbm, cm_ref), (pts_hbm, pts_ref), (inv_hbm, inv)]
        )
    ]
    for load in loads:
        load.start()
    for load in loads[:3]:
        load.wait()
    p = p_ref[0]

    base = jnp.clip(first_slot(p, row) - 1, 0, pts_ref.shape[0] - RW - 1)
    for t in range(3):
        wb[t, zl, y] = jnp.concatenate([pts_ref[base + 1 + t, 0], pts_ref[base + 4 + t, 0]], axis=1)
    first = pts_ref[base + 1, 0].astype(F32)
    second = pts_ref[base + 2, 0].astype(F32)
    pivot = pts_ref[base, 0].astype(F32)
    cand = jnp.concatenate([first, second], axis=1)
    piv = jnp.concatenate([pivot, jnp.zeros_like(pivot)], axis=1)
    for h in range(2):
        rows = slice(8 * h, 8 * h + 8)
        xe[h, 0] = cand[rows].astype(BF)
        xe[h, 1] = piv[rows].astype(BF)
    xb[q] = xe[core]
    cms[zl] = jnp.full((8, 128), cm_ref[0], jnp.int32).astype(F32)
    pl.semaphore_wait(barrier, len(q_peers) + len(y_peers) + len(line) - 1)

    sends = []

    def send(src, dst, ssem, rsem, to):
        copy = pltpu.make_async_remote_copy(
            src_ref=src, dst_ref=dst, send_sem=ssem, recv_sem=rsem, device_id=to, device_id_type=MESH
        )
        copy.start()
        sends.append(copy)

    def arrived(dst, rsem):
        pltpu.make_async_remote_copy(
            src_ref=dst, dst_ref=dst, send_sem=rsem, recv_sem=rsem, device_id=dev(), device_id_type=MESH
        ).wait_recv()

    def send_line(src_of, dst, ssem, rsem):
        for z_, k_ in line:
            send(src_of(z_), dst.at[core, z], ssem.at[k_ * NZ + z_], rsem.at[core * NZ + z], z_dev(z_, k_))

    def line_arrived(dst, rsem):
        for z_, k_ in line:
            arrived(dst.at[k_, z_], rsem.at[k_ * NZ + z_])

    zfirst, yfirst = pl.ds(0, 2), pl.ds(2, 1)
    for q_ in q_peers:
        send(xe.at[q_ % 2], xb.at[q], x_s.at[q_], x_r.at[q], q_dev(q_))
    for l_ in l_peers:
        send(cms.at[zl], cms.at[zl], c_s.at[l_], c_r.at[zl], dev(zl_=l_))
    for y_ in y_peers:
        send(wb.at[yfirst, zl, y], wb.at[yfirst, zl, y], wy_s.at[y_], wy_r.at[y], dev(y_=y_))
    for l_ in l_peers:
        send(wb.at[zfirst, zl, y], wb.at[zfirst, zl, y], wz_s.at[l_], wz_r.at[zl], dev(zl_=l_))

    for q_ in q_peers:
        arrived(xb.at[q_], x_r.at[q_])
    mine = jnp.zeros((8, 128), F32)
    for k in range(NP):
        r = ((k // 2) * 2 + zh) * 2 + k % 2
        mine += jnp.where(r == p % N_ROW, xb[k, 1].astype(F32), 0.0)
    ps[...] = mine.astype(BF)
    yp[y] = mine.astype(BF)
    yc[y] = xb[:, 0]
    for y_ in y_peers:
        send(ps, yp.at[y], yp_s.at[y_], yp_r.at[y], dev(y_=y_))
    for y_ in y_peers:
        send(xb.at[:, 0], yc.at[y], yc_s.at[y_], yc_r.at[y], dev(y_=y_))

    for l_ in l_peers:
        arrived(wb.at[zfirst, l_, y], wz_r.at[l_])
    for y_ in y_peers:
        send(wb.at[zfirst, :, y], wb.at[zfirst, :, y], w2y_s.at[y_], w2y_r.at[y], dev(y_=y_))
    for y_ in y_peers:
        arrived(wb.at[yfirst, zl, y_], wy_r.at[y_])
    for l_ in l_peers:
        send(wb.at[yfirst, zl], wb.at[yfirst, zl], w2z_s.at[l_], w2z_r.at[zl], dev(zl_=l_))

    low = lax.broadcasted_iota(jnp.int32, (8, 128), 1) < DIM
    for y_ in y_peers:
        arrived(yp.at[y_], yp_r.at[y_])
    for k in range(4):
        zq[k] = packed_pair(yp[k].astype(F32), yp[k + 4].astype(F32), low).astype(BF)
    zp[core, z] = zq[...]
    send_line(lambda z_: zq, zp, zp_s, zp_r)

    for l_ in l_peers:
        arrived(cms.at[l_], c_r.at[l_])
    wanted = [cms[l_] for l_ in range(NZL)]
    ranks = []
    for k in range(NP):
        r = ((k // 2) * 2 + zh) * 2 + k % 2
        own = first_slot(p, r) * N_ROW + r - p - 1
        ranks.append(jnp.where(low, own, own + N_ROW).astype(F32))
    for y_ in y_peers:
        arrived(yc.at[y_], yc_r.at[y_])
    for k4 in range(4):
        chosen = [[], []]
        for i in range(2):
            tiles = [yc[k4 + 4 * i, k].astype(F32) for k in range(NP)]
            for l_ in range(NZL):
                total = jnp.zeros((8, 128), F32)
                for k in range(NP):
                    total = jnp.where(wanted[l_] == ranks[k], tiles[k], total)
                chosen[i].append(total + pltpu.roll(total, DIM, 1))
        for l_ in range(NZL):
            zs[l_, k4] = jnp.where(low, chosen[0][l_], chosen[1][l_]).astype(BF)
    zc[core, z] = zs[zl]
    send_line(lambda z_: zs.at[z_ % NZL], zc, zc_s, zc_r)

    line_arrived(zp, zp_r)
    pivots = assembled(zp)
    xp[...] = pivots.astype(BF)
    fill_rhs(pivots, rhs, bias)
    for l_ in l_peers:
        arrived(wb.at[yfirst, l_], w2z_r.at[l_])
    for y_ in y_peers:
        arrived(wb.at[zfirst, :, y_], w2y_r.at[y_])

    loads[3].wait()
    half_rows = NB // 2

    @pl.loop(0, RW)
    def _(slot):
        which, half = slot % 3, slot // 3
        for m in range(2):
            rows = slice(m * half_rows, (m + 1) * half_rows)
            here = wb[which, 2 * m : 2 * m + 2].reshape(half_rows, 128)
            norm = row_norm(here.astype(F32), half * DIM)
            kpanel = jnp.exp2(SCALE * dot(here, rhs[half]) - norm - bias[0:1]).astype(BF)
            panel[slot, rows, 0:half_rows] = dot_t(
                kpanel[:, 0:half_rows], inv[0:half_rows, 0:half_rows]
            ).astype(BF)
            panel[slot, rows, half_rows:NB] = dot_t(kpanel, inv[half_rows:NB]).astype(BF)

    line_arrived(zc, zc_r)
    for copy in sends:
        copy.wait_send()


def gathered(panel_index, column_map, points, inverse_factor):
    vmem = pl.BlockSpec(memory_space=pltpu.VMEM)
    hbm = pl.BlockSpec(memory_space=pltpu.HBM)
    dma = pltpu.SemaphoreType.DMA
    counts = [NP, NP, NZL, NZL, NY, NY, NZL, NZL, NY, NY, NZL, NZL, NY, NY, NY, NY] + [2 * NZ] * 4 + [4]
    return pl.pallas_call(
        gather_kernel,
        out_shape=[
            pltpu.VMEM((3, NZL, NY, 16, 128), BF),
            pltpu.VMEM((2, NZ, 4, 8, 128), BF),
            pltpu.VMEM((NB, 128), BF),
            pltpu.VMEM((RW, NB, NB), BF),
            pltpu.VMEM((NB, NB), BF),
        ],
        in_specs=[hbm] * 4,
        out_specs=[vmem] * 5,
        scratch_shapes=[
            pltpu.SMEM((1,), jnp.int32),
            pltpu.SMEM((1,), jnp.int32),
            pltpu.VMEM(points.shape, BF),
            pltpu.VMEM((2, 2, 8, 128), BF),
            pltpu.VMEM((NP, 2, 8, 128), BF),
            pltpu.VMEM((8, 128), BF),
            pltpu.VMEM((NY, NP, 8, 128), BF),
            pltpu.VMEM((NY, 8, 128), BF),
            pltpu.VMEM((NZL, 8, 128), F32),
            pltpu.VMEM((NZL, 4, 8, 128), BF),
            pltpu.VMEM((4, 8, 128), BF),
            pltpu.VMEM((2, NZ, 4, 8, 128), BF),
            pltpu.VMEM((2, 128, NB), BF),
            pltpu.VMEM((8, NB), F32),
        ]
        + [dma((n,)) for n in counts],
        compiler_params=pltpu.CompilerParams(collective_id=0, has_side_effects=True, vmem_limit_bytes=61100 << 10),
        name="gather_panel",
    )(panel_index, column_map, points, inverse_factor)


def tiles_kernel(
    p_hbm, cm_hbm, wb, zc, xp, inv, panel, panel_out, update_out, rhs, bias, lcol, p_ref, cm_ref, in_s
):
    slot = pl.program_id(0)
    row, col = lax.axis_index("row"), lax.axis_index("col")
    half_rows = NB // 2

    @pl.when(slot == 0)
    def _():
        loads = [
            pltpu.make_async_copy(p_hbm, p_ref, in_s.at[0]),
            pltpu.make_async_copy(cm_hbm, cm_ref, in_s.at[1]),
        ]
        for load in loads:
            load.start()
        fill_rhs(assembled(zc), rhs, bias)
        norm = row_norm(xp[...].astype(F32), 0)
        cross = jnp.exp2(SCALE * dot(xp[...], rhs[0]) - norm - bias[0:1]).astype(BF)
        lcol[0:half_rows] = dot(inv[0:half_rows, 0:half_rows], cross[0:half_rows]).astype(BF)
        lcol[half_rows:NB] = dot(inv[half_rows:NB], cross).astype(BF)
        start = pl.multiple_of(col * 16, 16)
        for a in range(RW):
            panel_out[a] = panel[a, pl.ds(start, 16)]
        for load in loads:
            load.wait()

    p = p_ref[0]
    which, half = slot % 3, slot // 3
    tile_row = (first_slot(p, row) + slot) * N_ROW + row
    jitter = jnp.where(tile_row == p + 1 + cm_ref[0], JITTER, 0.0)
    eye = lax.broadcasted_iota(jnp.int32, (128, 128), 0) == lax.broadcasted_iota(jnp.int32, (128, 128), 1)
    diagonal = jnp.where(eye, jitter, 0.0)
    for m in range(2):
        rows = slice(m * half_rows, (m + 1) * half_rows)
        here = wb[which, 2 * m : 2 * m + 2].reshape(half_rows, 128)
        norm = row_norm(here.astype(F32), half * DIM)
        tile = jnp.exp2(SCALE * dot(here, rhs[half]) - norm - bias[0:1])
        product = dot(panel[slot, rows], lcol[...])
        for i in range(2):
            sub = slice(i * 128, (i + 1) * 128)
            out_rows = slice(m * half_rows + i * 128, m * half_rows + (i + 1) * 128)
            for j in range(4):
                cols = slice(j * 128, (j + 1) * 128)
                value = tile[sub, cols]
                if j == 2 * m + i:
                    value = value + diagonal
                update_out[0, out_rows, cols] = (value - product[sub, cols]).astype(BF)


def tiles(panel_index, column_map, wb, zc, xp, inverse_factor, panel):
    vmem = pl.BlockSpec(memory_space=pltpu.VMEM)
    hbm = pl.BlockSpec(memory_space=pltpu.HBM)
    flops = 2 * NB * NB * (RW * (128 + NB) + 2 * NB)
    return pl.pallas_call(
        tiles_kernel,
        grid=(RW,),
        out_shape=[
            jax.ShapeDtypeStruct((RW, 16, NB), BF),
            jax.ShapeDtypeStruct((RW, NB, NB), BF),
        ],
        in_specs=[hbm, hbm, vmem, vmem, vmem, vmem, vmem],
        out_specs=[
            pl.BlockSpec((RW, 16, NB), lambda i: (0, 0, 0)),
            pl.BlockSpec((1, NB, NB), lambda i: (i, 0, 0)),
        ],
        scratch_shapes=[
            pltpu.VMEM((2, 128, NB), BF),
            pltpu.VMEM((8, NB), F32),
            pltpu.VMEM((NB, NB), BF),
            pltpu.SMEM((1,), jnp.int32),
            pltpu.SMEM((1,), jnp.int32),
            pltpu.SemaphoreType.DMA((2,)),
        ],
        compiler_params=pltpu.CompilerParams(vmem_limit_bytes=24 << 20),
        cost_estimate=pl.CostEstimate(flops=flops, bytes_accessed=5 << 20, transcendentals=7 * NB * NB),
        name="window_tiles",
    )(panel_index, column_map, wb, zc, xp, inverse_factor, panel)


def shards(points, inverse_factor, panel_index, column_map):
    wb, zc, xp, panel, inv = gathered(panel_index, column_map, points, inverse_factor)
    panel_part, update = tiles(panel_index, column_map, wb, zc, xp, inv, panel)
    return panel_part[:, None], update[:, None, :, None, :]


def solution(mesh):
    in_specs = (P(None, "row", "col", None), P(), P(), P("col"))
    out_specs = (P(None, "row", "col", None), P(None, "row", None, "col", None))
    return jax.shard_map(shards, mesh=mesh, in_specs=in_specs, out_specs=out_specs, check_vma=False)
```

time: 47.9 us -> 43.2 us (0.902)
  Pallas kernels: 45.7 us -> 41.1 us
    pallas_call x1, Pallas kernels: 9.45 us -> 5.73 us  [tiles(): pl.pallas_call(tiles_kernel, grid=(RW,), out_shape=[jax.ShapeDtypeStruct(...]
    pallas_call x1, Pallas kernels: 36.3 us -> 35.4 us  [gathered(): pl.pallas_call(gather_kernel, out_shape=[pltpu.VMEM((3, NZL, NY, 16, 128)...]
where the time goes in v2:
time: 43.2 us; the launch traced here: 43.1 us
  Pallas kernels  41.1 us (95%)
  between operations  1.93 us (4%)
    pallas_call x1, Pallas kernels, gathered(): pl.pallas_call(gather_kernel, out_shape=[pltpu.VMEM((3, NZL, NY, 16, 128)...  35.4 us
    pallas_call x1, Pallas kernels, tiles(): pl.pallas_call(tiles_kernel, grid=(RW,), out_shape=[jax.ShapeDtypeStruct(...  5.73 us

profile of v2, /device:TPU:1, one launch (start us, length us, event | category | flops | bytes accessed | tf_op | source)
XLA Modules:
  0.0 43.1 jit_solution(7165007321709571794)
XLA Ops:
  1.9 35.4 %gather_panel.1 = (bf16[3,4,8,16,128]{4,3,2,1,0:T(8,128)(2,1)S(1)}, bf16[2,8,4,8,128]{4,3,2,1,0:T(8,128)(2,1)S(1)}, bf16[512,128]{1,0:T(8,128)(2,1)S(1)}, bf16[6...) custom-call(s32[1]{0:T(128)S(6)} %copy.8.p_hbm, s32[1]{0:T(128)S(6)} %copy.9.cm_hbm, bf16[12,1,16,64]{3,2,1,0:T(8,128)(2,1)} %pts_hbm.1, ...), custom_call_target="tpu_custom_call" | custom-call | tf_op jit(solution)/shard_map/gather_panel/pallas_call | solution.py:251
  37.3 5.7 %window_tiles.1 = (bf16[6,16,512]{2,1,0:T(8,128)(2,1)}, bf16[6,512,512]{2,1,0:T(8,128)(2,1)}) custom-call(s32[1]{0:T(128)S(6)} %copy.8.p_hbm, s32[1]{0:T(128)S(6)} %copy.9.cm_hbm, bf16[3,4,8,16,128]{4,3,2,1,0:T(8,128)(2,1)S(1)} %get-tuple-element.9.wb, bf16[2,8,4,8,128]{4,3,2,1,0:T(8,128)(2,1)S(1)} %get-tuple-element.10.zc, ...), custom_call_target="tpu_custom_call" | custom-call | flops 2550136832 | bytes 5242880 | tf_op jit(solution)/shard_map/window_tiles/pallas_call | solution.py:337

commit v3 on v2

--- a/solution.py
+++ b/solution.py
@@ -67,7 +67,7 @@
     p_hbm, cm_hbm, pts_hbm, inv_hbm, wb, zc, xp, panel, inv,
     p_ref, cm_ref, pts_ref, xe, xb, ps, yc, yp, cms, zs, zq, zp, rhs, bias,
     x_s, x_r, c_s, c_r, wy_s, wy_r, wz_s, wz_r, w2y_s, w2y_r, w2z_s, w2z_r,
-    yc_s, yc_r, yp_s, yp_r, zp_s, zp_r, zc_s, zc_r, in_s,
+    yc_s, yc_r, yp_s, yp_r, zp_s, zp_r, zc_s, zc_r, in_s, rounds,
 ):
     row, col = lax.axis_index("row"), lax.axis_index("col")
     x, zh, core = row // 4, (row // 2) % 2, row % 2
@@ -89,14 +89,6 @@
     z_peers = [(z + d) % NZ for d in range(1, NZ)]
     l_peers = [(zl + d) % NZL for d in range(1, NZL)]
     line = [(z_, (core + k) % 2) for z_ in z_peers for k in range(2)] + [(z, 1 - core)]
-
-    barrier = pltpu.get_barrier_semaphore()
-    for q_ in q_peers:
-        pl.semaphore_signal(barrier, 1, device_id=q_dev(q_), device_id_type=MESH)
-    for y_ in y_peers:
-        pl.semaphore_signal(barrier, 1, device_id=dev(y_=y_), device_id_type=MESH)
-    for z_, k_ in line[:-1]:
-        pl.semaphore_signal(barrier, 1, device_id=z_dev(z_, k_), device_id_type=MESH)
 
     loads = [
         pltpu.make_async_copy(src, dst, in_s.at[i])
@@ -106,6 +98,15 @@
     ]
     for load in loads:
         load.start()
+
+    barrier = pltpu.get_barrier_semaphore()
+    y_near = [(y + 1) % NY, (y + NY - 1) % NY]
+    z_near = [(z + 1) % NZ, (z + NZ - 1) % NZ]
+    near = [dev(y_=y_) for y_ in y_near] + [z_dev(z_, core) for z_ in z_near]
+    greeted = [q_dev(q_) for q_ in q_peers] + near + [z_dev(z_, 1 - core) for z_ in z_near]
+    for to in greeted:
+        pl.semaphore_signal(barrier, 1, device_id=to, device_id_type=MESH)
+
     for load in loads[:3]:
         load.wait()
     p = p_ref[0]
@@ -124,7 +125,7 @@
         xe[h, 1] = piv[rows].astype(BF)
     xb[q] = xe[core]
     cms[zl] = jnp.full((8, 128), cm_ref[0], jnp.int32).astype(F32)
-    pl.semaphore_wait(barrier, len(q_peers) + len(y_peers) + len(line) - 1)
+    pl.semaphore_wait(barrier, len(greeted))
 
     sends = []
 
@@ -151,6 +152,10 @@
     zfirst, yfirst = pl.ds(0, 2), pl.ds(2, 1)
     for q_ in q_peers:
         send(xe.at[q_ % 2], xb.at[q], x_s.at[q_], x_r.at[q], q_dev(q_))
+    for k in range(NY // 2 - 1):
+        for to in near:
+            pl.semaphore_signal(rounds.at[k], 1, device_id=to, device_id_type=MESH)
+        pl.semaphore_wait(rounds.at[k], len(near))
     for l_ in l_peers:
         send(cms.at[zl], cms.at[zl], c_s.at[l_], c_r.at[zl], dev(zl_=l_))
     for y_ in y_peers:
@@ -275,7 +280,8 @@
             pltpu.VMEM((2, 128, NB), BF),
             pltpu.VMEM((8, NB), F32),
         ]
-        + [dma((n,)) for n in counts],
+        + [dma((n,)) for n in counts]
+        + [pltpu.SemaphoreType.REGULAR((NY // 2 - 1,))],
         compiler_params=pltpu.CompilerParams(collective_id=0, has_side_effects=True, vmem_limit_bytes=61100 << 10),
         name="gather_panel",
     )(panel_index, column_map, points, inverse_factor)

time: 43.2 us -> 46.5 us (1.076)
  Pallas kernels: 41.1 us -> 44.4 us
    pallas_call x1, Pallas kernels: 35.4 us -> 38.7 us  [gathered(): pl.pallas_call(gather_kernel, out_shape=[pltpu.VMEM((3, NZL, NY, 16, 128)...]
where the time goes in v3:
time: 46.5 us; the launch traced here: 46.4 us
  Pallas kernels  44.4 us (95%)
  between operations  1.93 us (4%)
    pallas_call x1, Pallas kernels, gathered(): pl.pallas_call(gather_kernel, out_shape=[pltpu.VMEM((3, NZL, NY, 16, 128)...  38.7 us
    pallas_call x1, Pallas kernels, tiles(): pl.pallas_call(tiles_kernel, grid=(RW,), out_shape=[jax.ShapeDtypeStruct(...  5.72 us

profile of v3, /device:TPU:1, one launch (start us, length us, event | category | flops | bytes accessed | tf_op | source)
XLA Modules:
  0.0 46.4 jit_solution(2589606705555507658)
XLA Ops:
  1.9 38.7 %gather_panel.1 = (bf16[3,4,8,16,128]{4,3,2,1,0:T(8,128)(2,1)S(1)}, bf16[2,8,4,8,128]{4,3,2,1,0:T(8,128)(2,1)S(1)}, bf16[512,128]{1,0:T(8,128)(2,1)S(1)}, bf16[6...) custom-call(s32[1]{0:T(128)S(6)} %copy.8.p_hbm, s32[1]{0:T(128)S(6)} %copy.9.cm_hbm, bf16[12,1,16,64]{3,2,1,0:T(8,128)(2,1)} %pts_hbm.1, ...), custom_call_target="tpu_custom_call" | custom-call | tf_op jit(solution)/shard_map/gather_panel/pallas_call | solution.py:256
  40.6 5.7 %window_tiles.1 = (bf16[6,16,512]{2,1,0:T(8,128)(2,1)}, bf16[6,512,512]{2,1,0:T(8,128)(2,1)}) custom-call(s32[1]{0:T(128)S(6)} %copy.8.p_hbm, s32[1]{0:T(128)S(6)} %copy.9.cm_hbm, bf16[3,4,8,16,128]{4,3,2,1,0:T(8,128)(2,1)S(1)} %get-tuple-element.9.wb, bf16[2,8,4,8,128]{4,3,2,1,0:T(8,128)(2,1)S(1)} %get-tuple-element.10.zc, ...), custom_call_target="tpu_custom_call" | custom-call | flops 2550136832 | bytes 5242880 | tf_op jit(solution)/shard_map/window_tiles/pallas_call | solution.py:343

commit v4 on v2

--- a/solution.py
+++ b/solution.py
@@ -64,7 +64,7 @@
 
 
 def gather_kernel(
-    p_hbm, cm_hbm, pts_hbm, inv_hbm, wb, zc, xp, panel, inv,
+    p_hbm, cm_hbm, pts_hbm, inv_hbm, wb, zc, xp, panel, inv, mark,
     p_ref, cm_ref, pts_ref, xe, xb, ps, yc, yp, cms, zs, zq, zp, rhs, bias,
     x_s, x_r, c_s, c_r, wy_s, wy_r, wz_s, wz_r, w2y_s, w2y_r, w2z_s, w2z_r,
     yc_s, yc_r, yp_s, yp_r, zp_s, zp_r, zc_s, zc_r, in_s,
@@ -85,18 +85,10 @@
         return dev(zh_=z_ // NZL, zl_=z_ % NZL, core_=core_)
 
     q_peers = [(q + d) % NP for d in range(1, NP)]
-    y_peers = [(y + d) % NY for d in range(1, NY)]
-    z_peers = [(z + d) % NZ for d in range(1, NZ)]
+    y_peers = [(y + d) % NY for d in (4, 3, 5, 2, 6, 1, 7)]
+    z_peers = [(z + d) % NZ for d in (4, 3, 5, 2, 6, 1, 7)]
     l_peers = [(zl + d) % NZL for d in range(1, NZL)]
     line = [(z_, (core + k) % 2) for z_ in z_peers for k in range(2)] + [(z, 1 - core)]
-
-    barrier = pltpu.get_barrier_semaphore()
-    for q_ in q_peers:
-        pl.semaphore_signal(barrier, 1, device_id=q_dev(q_), device_id_type=MESH)
-    for y_ in y_peers:
-        pl.semaphore_signal(barrier, 1, device_id=dev(y_=y_), device_id_type=MESH)
-    for z_, k_ in line[:-1]:
-        pl.semaphore_signal(barrier, 1, device_id=z_dev(z_, k_), device_id_type=MESH)
 
     loads = [
         pltpu.make_async_copy(src, dst, in_s.at[i])
@@ -106,6 +98,12 @@
     ]
     for load in loads:
         load.start()
+
+    barrier = pltpu.get_barrier_semaphore()
+    greeted = [z_dev(z_, k_) for z_, k_ in line[:-1]] + [dev(y_=y_) for y_ in y_peers] + [q_dev(q_) for q_ in q_peers]
+    for to in greeted:
+        pl.semaphore_signal(barrier, 1, device_id=to, device_id_type=MESH)
+
     for load in loads[:3]:
         load.wait()
     p = p_ref[0]
@@ -124,7 +122,8 @@
         xe[h, 1] = piv[rows].astype(BF)
     xb[q] = xe[core]
     cms[zl] = jnp.full((8, 128), cm_ref[0], jnp.int32).astype(F32)
-    pl.semaphore_wait(barrier, len(q_peers) + len(y_peers) + len(line) - 1)
+    mark[...] = jnp.full((8, 128), p + 1 + cm_ref[0] - row - first_slot(p, row) * N_ROW, jnp.int32)
+    pl.semaphore_wait(barrier, len(greeted))
 
     sends = []
 
@@ -187,6 +186,7 @@
     for k in range(4):
         zq[k] = packed_pair(yp[k].astype(F32), yp[k + 4].astype(F32), low).astype(BF)
     zp[core, z] = zq[...]
+    early = len(sends)
     send_line(lambda z_: zq, zp, zp_s, zp_r)
 
     for l_ in l_peers:
@@ -213,6 +213,8 @@
     zc[core, z] = zs[zl]
     send_line(lambda z_: zs.at[z_ % NZL], zc, zc_s, zc_r)
 
+    for copy in sends[:early]:
+        copy.wait_send()
     line_arrived(zp, zp_r)
     pivots = assembled(zp)
     xp[...] = pivots.astype(BF)
@@ -239,7 +241,7 @@
             panel[slot, rows, half_rows:NB] = dot_t(kpanel, inv[half_rows:NB]).astype(BF)
 
     line_arrived(zc, zc_r)
-    for copy in sends:
+    for copy in sends[early:]:
         copy.wait_send()
 
 
@@ -256,9 +258,10 @@
             pltpu.VMEM((NB, 128), BF),
             pltpu.VMEM((RW, NB, NB), BF),
             pltpu.VMEM((NB, NB), BF),
+            pltpu.VMEM((8, 128), jnp.int32),
         ],
         in_specs=[hbm] * 4,
-        out_specs=[vmem] * 5,
+        out_specs=[vmem] * 6,
         scratch_shapes=[
             pltpu.SMEM((1,), jnp.int32),
             pltpu.SMEM((1,), jnp.int32),
@@ -281,21 +284,13 @@
     )(panel_index, column_map, points, inverse_factor)
 
 
-def tiles_kernel(
-    p_hbm, cm_hbm, wb, zc, xp, inv, panel, panel_out, update_out, rhs, bias, lcol, p_ref, cm_ref, in_s
-):
+def tiles_kernel(mark, wb, zc, xp, inv, panel, panel_out, update_out, rhs, bias, lcol):
     slot = pl.program_id(0)
-    row, col = lax.axis_index("row"), lax.axis_index("col")
+    col = lax.axis_index("col")
     half_rows = NB // 2
 
     @pl.when(slot == 0)
     def _():
-        loads = [
-            pltpu.make_async_copy(p_hbm, p_ref, in_s.at[0]),
-            pltpu.make_async_copy(cm_hbm, cm_ref, in_s.at[1]),
-        ]
-        for load in loads:
-            load.start()
         fill_rhs(assembled(zc), rhs, bias)
         norm = row_norm(xp[...].astype(F32), 0)
         cross = jnp.exp2(SCALE * dot(xp[...], rhs[0]) - norm - bias[0:1]).astype(BF)
@@ -304,35 +299,29 @@
         start = pl.multiple_of(col * 16, 16)
         for a in range(RW):
             panel_out[a] = panel[a, pl.ds(start, 16)]
-        for load in loads:
-            load.wait()
-
-    p = p_ref[0]
     which, half = slot % 3, slot // 3
-    tile_row = (first_slot(p, row) + slot) * N_ROW + row
-    jitter = jnp.where(tile_row == p + 1 + cm_ref[0], JITTER, 0.0)
+    here_too = mark[0:1] == slot * N_ROW
     eye = lax.broadcasted_iota(jnp.int32, (128, 128), 0) == lax.broadcasted_iota(jnp.int32, (128, 128), 1)
-    diagonal = jnp.where(eye, jitter, 0.0)
-    for m in range(2):
-        rows = slice(m * half_rows, (m + 1) * half_rows)
-        here = wb[which, 2 * m : 2 * m + 2].reshape(half_rows, 128)
-        norm = row_norm(here.astype(F32), half * DIM)
-        tile = jnp.exp2(SCALE * dot(here, rhs[half]) - norm - bias[0:1])
-        product = dot(panel[slot, rows], lcol[...])
-        for i in range(2):
+    diagonal = jnp.where(eye & here_too, JITTER, 0.0)
+    here = wb[which].reshape(NB, 128)
+    norm = row_norm(here.astype(F32), half * DIM)
+    for n in range(2):
+        side = slice(n * half_rows, (n + 1) * half_rows)
+        tile = jnp.exp2(SCALE * dot(here, rhs[half, :, side]) - norm - bias[0:1, side])
+        product = dot(panel[slot], lcol[:, side])
+        for i in range(4):
             sub = slice(i * 128, (i + 1) * 128)
-            out_rows = slice(m * half_rows + i * 128, m * half_rows + (i + 1) * 128)
-            for j in range(4):
+            for j in range(2):
                 cols = slice(j * 128, (j + 1) * 128)
                 value = tile[sub, cols]
-                if j == 2 * m + i:
+                if 2 * n + j == i:
                     value = value + diagonal
-                update_out[0, out_rows, cols] = (value - product[sub, cols]).astype(BF)
-
-
-def tiles(panel_index, column_map, wb, zc, xp, inverse_factor, panel):
+                out_cols = slice(n * half_rows + j * 128, n * half_rows + (j + 1) * 128)
+                update_out[0, sub, out_cols] = (value - product[sub, cols]).astype(BF)
+
+
+def tiles(mark, wb, zc, xp, inverse_factor, panel):
     vmem = pl.BlockSpec(memory_space=pltpu.VMEM)
-    hbm = pl.BlockSpec(memory_space=pltpu.HBM)
     flops = 2 * NB * NB * (RW * (128 + NB) + 2 * NB)
     return pl.pallas_call(
         tiles_kernel,
@@ -341,7 +330,7 @@
             jax.ShapeDtypeStruct((RW, 16, NB), BF),
             jax.ShapeDtypeStruct((RW, NB, NB), BF),
         ],
-        in_specs=[hbm, hbm, vmem, vmem, vmem, vmem, vmem],
+        in_specs=[vmem] * 6,
         out_specs=[
             pl.BlockSpec((RW, 16, NB), lambda i: (0, 0, 0)),
             pl.BlockSpec((1, NB, NB), lambda i: (i, 0, 0)),
@@ -350,19 +339,16 @@
             pltpu.VMEM((2, 128, NB), BF),
             pltpu.VMEM((8, NB), F32),
             pltpu.VMEM((NB, NB), BF),
-            pltpu.SMEM((1,), jnp.int32),
-            pltpu.SMEM((1,), jnp.int32),
-            pltpu.SemaphoreType.DMA((2,)),
         ],
         compiler_params=pltpu.CompilerParams(vmem_limit_bytes=24 << 20),
         cost_estimate=pl.CostEstimate(flops=flops, bytes_accessed=5 << 20, transcendentals=7 * NB * NB),
         name="window_tiles",
-    )(panel_index, column_map, wb, zc, xp, inverse_factor, panel)
+    )(mark, wb, zc, xp, inverse_factor, panel)
 
 
 def shards(points, inverse_factor, panel_index, column_map):
-    wb, zc, xp, panel, inv = gathered(panel_index, column_map, points, inverse_factor)
-    panel_part, update = tiles(panel_index, column_map, wb, zc, xp, inv, panel)
+    wb, zc, xp, panel, inv, mark = gathered(panel_index, column_map, points, inverse_factor)
+    panel_part, update = tiles(mark, wb, zc, xp, inv, panel)
     return panel_part[:, None], update[:, None, :, None, :]
 
 

time: 43.2 us -> 42.4 us (0.981)
  Pallas kernels: 41.1 us -> 40.3 us
    pallas_call x1, Pallas kernels: 35.4 us -> 34.6 us  [gathered(): pl.pallas_call(gather_kernel, out_shape=[pltpu.VMEM((3, NZL, NY, 16, 128)...]
where the time goes in v4:
time: 42.4 us; the launch traced here: 42.2 us
  Pallas kernels  40.3 us (95%)
  between operations  1.93 us (5%)
    pallas_call x1, Pallas kernels, gathered(): pl.pallas_call(gather_kernel, out_shape=[pltpu.VMEM((3, NZL, NY, 16, 128)...  34.6 us
    pallas_call x1, Pallas kernels, tiles(): pl.pallas_call(tiles_kernel, grid=(RW,), out_shape=[jax.ShapeDtypeStruct(...  5.65 us

profile of v4, /device:TPU:1, one launch (start us, length us, event | category | flops | bytes accessed | tf_op | source)
XLA Modules:
  0.0 42.2 jit_solution(3455657054095811589)
XLA Ops:
  1.9 34.6 %gather_panel.1 = (bf16[3,4,8,16,128]{4,3,2,1,0:T(8,128)(2,1)S(1)}, bf16[2,8,4,8,128]{4,3,2,1,0:T(8,128)(2,1)S(1)}, bf16[512,128]{1,0:T(8,128)(2,1)S(1)}, bf16[6...) custom-call(s32[1]{0:T(128)S(6)} %copy.8.p_hbm, s32[1]{0:T(128)S(6)} %copy.9.cm_hbm, ...), custom_call_target="tpu_custom_call" | custom-call | tf_op jit(solution)/shard_map/gather_panel/pallas_call | solution.py:253
  36.6 5.7 %window_tiles.1 = (bf16[6,16,512]{2,1,0:T(8,128)(2,1)}, bf16[6,512,512]{2,1,0:T(8,128)(2,1)}) custom-call(s32[8,128]{1,0:T(8,128)S(1)} %get-tuple-element.10.mark, bf16[3,4,8,16,128]{4,3,2,1,0:T(8,128)(2,1)S(1)} %get-tuple-element.11.wb, bf16[2,8,4,8,128]{4,3,2,1,0:T(8,128)(2,1)S(1)} %get-tuple-element.12.zc, bf16[512,128]{1,0:T(8,128)(2,1)S(1)} %get-tuple-element.13.xp, ...), custom_call_target="tpu_custom_call" | custom-call | flops 2550136832 | bytes 5242880 | tf_op jit(solution)/shard_map/window_tiles/pallas_call | solution.py:326
